TPU v7x, 32 devices: a whole 2x2x4 slice. The times are simulated.
32 devices in a mesh: seq: 32 (over z, y, x, core).
Axes of the slice: x: 2, y: 2, z: 4, core: 2. Of those that a mesh axis runs over, the one named last changes fastest.
Arguments:
- history: float32 [12288, 1024], P('seq'), may hold values from -6 to 6
- taps: float32 [12288, 1024], P('seq'), may hold values from -0.109375 to 0.109375
- self_taps: float32 [1024, 256], P('seq'), may hold values from -0.375 to 0.375
- fresh: float32 [1024, 256], P('seq'), may hold values from -6 to 6
- gate: float32 [1024, 256], P('seq'), may hold values from -6 to 6
Outputs:
- gated: float32 [1024, 256], P('seq')
All inputs are finite; a program needn't handle non-finite values.
Results may differ from a plain program's by a relative error of at most 0.000053.
Values sent between devices are 32-bit elements; how exact they have to be, the bound alone decides.
A program may use at most 64 MiB of HBM per device.

v0:
```python
import math

import jax
import jax.numpy as jnp
import numpy as np
from jax import lax
from jax.experimental import pallas as pl
from jax.experimental.pallas import tpu as pltpu
from jax.sharding import PartitionSpec as P

AXIS = "seq"
PLANE = 8
MESH = pl.DeviceIdType.MESH
F32 = jnp.float32
BF16 = jnp.bfloat16


def dft_matrix(seg):
    phase = np.outer(4 * np.arange(seg) + 1, np.arange(seg)) % (4 * seg)
    angle = phase * (math.pi / (2 * seg))
    return np.concatenate([np.cos(angle), -np.sin(angle)], axis=0)


def halves(matrix):
    high = np.asarray(matrix, np.float32).astype(BF16)
    low = np.asarray(matrix - high.astype(np.float64), np.float32).astype(BF16)
    return high, low


def split(value):
    high = value.astype(BF16)
    return high, (value - high.astype(F32)).astype(BF16)


def mul_conj(a, b):
    return a[0] * b[0] + a[1] * b[1], a[1] * b[0] - a[0] * b[1]


def mul(a, b):
    return a[0] * b[0] - a[1] * b[1], a[0] * b[1] + a[1] * b[0]


def add(a, b):
    return a[0] + b[0], a[1] + b[1]


def turn(a):
    return -a[1], a[0]


def back(a):
    return a[1], -a[0]


def local_products(hs, ts):
    us = [None] + [add(ts[a], turn(ts[a - 1])) for a in range(1, len(ts))]
    first = mul_conj(hs[0], ts[0])
    for a in range(1, len(hs)):
        first = add(first, mul_conj(hs[a], us[a]))
    second = mul_conj(hs[1], ts[0])
    for a in range(2, len(hs)):
        second = add(second, mul_conj(hs[a], us[a - 1]))
    return first, second


def halo_products(first, second, h0, h1, t_near, t_before, h_after):
    one = mul_conj(h0, t_before)
    two = add(mul_conj(h1, t_before), mul_conj(h_after, t_near))
    return add(first, back(one)), add(add(second, one), back(two))


def own_products(f0, f1, s0, s1):
    first = mul(f0, s0)
    return first, add(turn(first), add(mul(f0, s1), mul(f1, s0)))


def plain_body(history, taps, self_taps, fresh, gate):
    n = lax.axis_size(AXIS)
    seg = fresh.shape[1] // 2
    matrix = jnp.asarray(dft_matrix(seg).astype(np.float32))
    hp = lax.Precision.HIGHEST
    before = lax.ppermute(taps[-seg:], AXIS, [(s, s + 1) for s in range(n - 1)])
    after = lax.ppermute(history[:seg], AXIS, [(s, s - 1) for s in range(1, n)])

    def forward(rows):
        spec = jnp.dot(matrix, rows, precision=hp)
        return spec[:seg], spec[seg:]

    def inverse(spec):
        return jnp.dot(matrix.T / seg, jnp.concatenate(spec, axis=0), precision=hp)

    count = history.shape[0] // seg
    hs = [forward(history[a * seg : (a + 1) * seg]) for a in range(count)]
    ts = [forward(taps[a * seg : (a + 1) * seg]) for a in range(count)]
    first, second = local_products(hs, ts)
    first, second = halo_products(first, second, hs[0], hs[1], ts[-2], forward(before), forward(after))
    part = jnp.concatenate([inverse(first), inverse(second)], axis=0).T
    summed = lax.psum_scatter(part, AXIS, scatter_dimension=0, tiled=True)
    f, s = fresh.T, self_taps.T
    own = own_products(forward(f[:seg]), forward(f[seg:]), forward(s[:seg]), forward(s[seg:]))
    own_part = jnp.concatenate([inverse(own[0]), inverse(own[1])], axis=0).T
    return gate * (summed + own_part)


def kernel(n, seg, hist, taps, self_taps, fresh, gate, fh, fl, gh, gl, out,
           hist_v, taps_v, tb, ha, sh0, sh1, st1, q0, q1, parts, d_recv, p_send, p_recv, z_send, z_recv,
           load_sem, tb_s, tb_r, ha_s, ha_r, d_s, d_r, p_s, p_r, z_s, z_r):
    me = lax.axis_index(AXIS)
    nz = n // PLANE
    my_z, low = me // PLANE, me % PLANE
    core, spot = me % 2, low // 2
    rows = hist.shape[0]
    count = rows // seg
    width = hist.shape[1] // nz
    block = width // PLANE
    partner = me + 1 - 2 * core
    chips = PLANE // 2

    def lanes(z, i):
        return pl.ds(pl.multiple_of(((z + 1 + i) % nz) * width, width), width)

    def plane_peer(j):
        bit0, bit1 = spot % 2, spot // 2
        other = (bit0 + j % 2) % 2 + 2 * ((bit1 + j // 2) % 2)
        return other, me - low + other * 2 + core

    def remote(src, dst, send, recv, dev):
        return pltpu.make_async_remote_copy(
            src_ref=src, dst_ref=dst, send_sem=send, recv_sem=recv, device_id=(dev,), device_id_type=MESH
        )

    loads = []
    for i in range(nz):
        for k, (src, dst) in enumerate(((hist, hist_v), (taps, taps_v))):
            copy = pltpu.make_async_copy(src.at[:, lanes(my_z, i)], dst.at[i], load_sem.at[k, i])
            copy.start()
            loads.append(copy)

    outer = (me + 2 * core - 1 + n) % n
    peers = [partner, outer]
    peers += [plane_peer(j)[1] for j in range(1, chips)]
    peers += [(me + k * PLANE) % n for k in range(1, nz)]
    barrier = pltpu.get_barrier_semaphore()
    for peer in peers:
        pl.semaphore_signal(barrier, inc=1, device_id=(peer,), device_id_type=MESH)
    pl.semaphore_wait(barrier, len(peers))

    def taps_copy(i, z, dev):
        return remote(taps.at[pl.ds(rows - seg, seg), lanes(z, i)], tb.at[i], tb_s.at[i], tb_r.at[i], dev)

    def hist_copy(i, z, dev):
        return remote(hist.at[pl.ds(0, seg), lanes(z, i)], ha.at[i], ha_s.at[i], ha_r.at[i], dev)

    has_next, has_prev = me < n - 1, me > 0
    for i in range(nz):
        @pl.when(has_next)
        def _(i=i):
            taps_copy(i, (me + 1) // PLANE, me + 1).start()

        @pl.when(has_prev)
        def _(i=i):
            hist_copy(i, (me - 1) // PLANE, me - 1).start()

    def forward(value):
        both = jnp.concatenate(split(value), axis=0)
        spec = jnp.dot(fh[...], both, preferred_element_type=F32) + jnp.dot(
            fl[...], both, preferred_element_type=F32
        )
        return spec[:seg], spec[seg:]

    def keep(ref, i, spec):
        ref[i, :seg], ref[i, seg:] = spec

    def held(ref, i):
        return ref[i, :seg], ref[i, seg:]

    @pl.when(me == 0)
    def _():
        tb[...] = jnp.zeros_like(tb)

    @pl.when(me == n - 1)
    def _():
        ha[...] = jnp.zeros_like(ha)

    for i in range(nz):
        loads[2 * i].wait()
        loads[2 * i + 1].wait()
        hs = [forward(hist_v[i, pl.ds(a * seg, seg)]) for a in range(count)]
        ts = [forward(taps_v[i, pl.ds(a * seg, seg)]) for a in range(count)]
        first, second = local_products(hs, ts)
        keep(sh0, i, hs[0])
        keep(sh1, i, hs[1])
        keep(st1, i, ts[-2])
        keep(q0, i, first)
        keep(q1, i, second)

    contract = (((1,), (1,)), ((), ()))

    def dot_t(a, b):
        return lax.dot_general(a, b, contract, preferred_element_type=F32)

    f, s = fresh[...], self_taps[...]
    both = jnp.concatenate(split(jnp.concatenate([f[:, :seg], f[:, seg:], s[:, :seg], s[:, seg:]], axis=0)), axis=1)
    spec = dot_t(both, fh[...]) + dot_t(both, fl[...])
    pieces = [(spec[k * block : (k + 1) * block, :seg], spec[k * block : (k + 1) * block, seg:]) for k in range(4)]
    a, b = own_products(*pieces)
    high, low_half = split(jnp.concatenate([jnp.concatenate(a, axis=1), jnp.concatenate(b, axis=1)], axis=0))
    res = dot_t(high, gh[...]) + dot_t(low_half, gh[...]) + dot_t(high, gl[...])
    own = jnp.concatenate([res[:block], res[block:]], axis=1)

    def inverse(spec):
        hi, lo = split(jnp.concatenate(spec, axis=0))
        return (
            jnp.dot(gh[...], hi, preferred_element_type=F32)
            + jnp.dot(gh[...], lo, preferred_element_type=F32)
            + jnp.dot(gl[...], hi, preferred_element_type=F32)
        ).T

    def chip_copy(i):
        return remote(parts.at[i, 1 - core], d_recv.at[i], d_s.at[i], d_r.at[i], partner)

    def plane_copy(i, j):
        other, dev = plane_peer(j)
        return remote(p_send.at[i, other], p_recv.at[i, j - 1], p_s.at[i, j - 1], p_r.at[i, j - 1], dev)

    def z_copy(i):
        return remote(z_send.at[i], z_recv.at[i], z_s.at[i], z_r.at[i], (me + (i + 1) * PLANE) % n)

    def step_compute(i):
        @pl.when(has_prev)
        def _():
            taps_copy(i, my_z, me).wait_recv()

        @pl.when(has_next)
        def _():
            hist_copy(i, my_z, me).wait_recv()

        first, second = halo_products(
            held(q0, i), held(q1, i), held(sh0, i), held(sh1, i), held(st1, i), forward(tb[i]), forward(ha[i])
        )
        for half, spec in enumerate((first, second)):
            res = inverse(spec)
            for p in range(chips):
                for c in range(2):
                    at = (p * 2 + c) * block
                    parts[i, c, p, :, pl.ds(half * seg, seg)] = res[at : at + block]
        chip_copy(i).start()

    def step_plane(i):
        chip_copy(i).wait_recv()
        p_send[i] = parts[i, core] + d_recv[i]
        for j in range(1, chips):
            plane_copy(i, j).start()

    def step_z(i):
        for j in range(1, chips):
            plane_copy(i, j).wait_recv()
        total = p_send[i, spot]
        for j in range(1, chips):
            total = total + p_recv[i, j - 1]
        z_send[i] = total
        if i < nz - 1:
            z_copy(i).start()

    for i in range(nz + 2):
        if i < nz:
            step_compute(i)
        if 0 <= i - 1 < nz:
            step_plane(i - 1)
        if 0 <= i - 2 < nz:
            step_z(i - 2)

    total = z_send[nz - 1]
    for i in range(nz - 1):
        z_copy(i).wait_recv()
        total = total + z_recv[i]
    out[...] = gate[...] * (total + own)

    for i in range(nz):
        @pl.when(has_next)
        def _(i=i):
            taps_copy(i, (me + 1) // PLANE, me + 1).wait_send()

        @pl.when(has_prev)
        def _(i=i):
            hist_copy(i, (me - 1) // PLANE, me - 1).wait_send()

        chip_copy(i).wait_send()
        for j in range(1, chips):
            plane_copy(i, j).wait_send()
        if i < nz - 1:
            z_copy(i).wait_send()


def kernel_body(history, taps, self_taps, fresh, gate):
    n = lax.axis_size(AXIS)
    rows, channels = history.shape
    block, new_len = fresh.shape
    seg = new_len // 2
    nz = n // PLANE
    width = channels // nz
    fh, fl = halves(dft_matrix(seg))
    gh, gl = halves(dft_matrix(seg).T / seg)
    fh, fl = np.concatenate([fh, fh], axis=1), np.concatenate([fl, fl], axis=1)
    vmem = pl.BlockSpec(memory_space=pltpu.VMEM)
    hbm = pl.BlockSpec(memory_space=pl.ANY)
    chips = PLANE // 2
    dma = pltpu.SemaphoreType.DMA
    spec = pltpu.VMEM((nz, 2 * seg, width), F32)
    return pl.pallas_call(
        lambda *refs: kernel(n, seg, *refs),
        out_shape=jax.ShapeDtypeStruct(fresh.shape, F32),
        in_specs=[hbm, hbm] + [vmem] * 7,
        out_specs=vmem,
        scratch_shapes=[
            pltpu.VMEM((nz, rows, width), F32),
            pltpu.VMEM((nz, rows, width), F32),
            pltpu.VMEM((nz, seg, width), F32),
            pltpu.VMEM((nz, seg, width), F32),
            spec, spec, spec, spec, spec,
            pltpu.VMEM((nz, 2, chips, block, new_len), F32),
            pltpu.VMEM((nz, chips, block, new_len), F32),
            pltpu.VMEM((nz, chips, block, new_len), F32),
            pltpu.VMEM((nz, chips - 1, block, new_len), F32),
            pltpu.VMEM((nz, block, new_len), F32),
            pltpu.VMEM((nz - 1, block, new_len), F32),
            dma((2, nz)),
            dma((nz,)), dma((nz,)), dma((nz,)), dma((nz,)),
            dma((nz,)), dma((nz,)),
            dma((nz, chips - 1)), dma((nz, chips - 1)),
            dma((nz - 1,)), dma((nz - 1,)),
        ],
        compiler_params=pltpu.CompilerParams(collective_id=0, has_side_effects=True),
        name="hyena",
    )(history, taps, self_taps, fresh, gate, *(jnp.asarray(m) for m in (fh, fl, gh, gl)))


def solution(mesh):
    n = mesh.shape[AXIS]

    def body(history, taps, self_taps, fresh, gate):
        channels = history.shape[1]
        block = fresh.shape[0]
        fits = n % PLANE == 0 and n > PLANE and block % 8 == 0 and (block * PLANE) % 128 == 0
        chosen = kernel_body if fits and channels == block * n else plain_body
        return chosen(history, taps, self_taps, fresh, gate)

    spec = P(AXIS, None)
    return jax.shard_map(body, mesh=mesh, in_specs=(spec,) * 5, out_specs=spec, check_vma=False)
```

profile of v0, /device:TPU:0, one launch (start us, length us, event | category | flops | bytes accessed | tf_op | source)
XLA Modules:
  0.0 32.7 jit_solution(11878616334474616051)
XLA Ops:
  0.0 31.4 %hyena.1 = f32[32,256]{1,0:T(8,128)} custom-call(f32[384,1024]{1,0:T(8,128)} %refs_0_.1, f32[384,1024]{1,0:T(8,128)} %refs_1_.1, f32[32,256]{1,0:T(8,128)} %refs_2_.1, f32[32,256]{1,0:T(8,128)} %refs_3_.1, f32[32,256]{1,0:T(8,128)} %refs_4_.1, bf16[256,256]{1,0:T(8,128)(2,1)} %constant.8.clone.refs_5_, bf16[256,256]{1,0:T(8,128)(2,1)} %constant.9.clone.refs_6_, ...), custom_call_target="tpu_custom_call" | custom-call | tf_op jit(solution)/shard_map/hyena/pallas_call | solution.py:310
  31.4 1.4 %copy.11 = f32[32,256]{1,0:T(8,128)} copy(f32[32,256]{1,0:T(8,128)} %hyena.1) | data formatting | bytes 65536
where the time goes:
time: 32.9 us; the launch traced here: 32.7 us
  Pallas kernels  31.4 us (95%)
  local copies, waits for them, and re-layouts  1.38 us (4%)
    pallas_call x1, Pallas kernels, kernel_body(): pl.pallas_call(lambda *refs: kernel(n, seg, *refs), out_shape=jax.ShapeDt...  31.4 us
    unnamed x1, local copies, waits for them, and re-layouts  1.38 us

commit v1 on v0

--- a/solution.py
+++ b/solution.py
@@ -102,9 +102,9 @@
     return gate * (summed + own_part)
 
 
-def kernel(n, seg, hist, taps, self_taps, fresh, gate, fh, fl, gh, gl, out,
-           hist_v, taps_v, tb, ha, sh0, sh1, st1, q0, q1, parts, d_recv, p_send, p_recv, z_send, z_recv,
-           load_sem, tb_s, tb_r, ha_s, ha_r, d_s, d_r, p_s, p_r, z_s, z_r):
+def kernel(n, seg, hist, taps, self_taps_h, fresh_h, gate_h, fh_h, fl_h, gh_h, gl_h, out,
+           self_taps, fresh, gate, fh, fl, gh, gl, hist_v, taps_v, tb, ha, sh0, sh1, st1, q0, q1, parts, d_recv, p_send, p_recv, z_send, z_recv,
+           small_sem, load_sem, tb_s, tb_r, ha_s, ha_r, d_s, d_r, p_s, p_r, z_s, z_r):
     me = lax.axis_index(AXIS)
     nz = n // PLANE
     my_z, low = me // PLANE, me % PLANE
@@ -129,6 +129,28 @@
             src_ref=src, dst_ref=dst, send_sem=send, recv_sem=recv, device_id=(dev,), device_id_type=MESH
         )
 
+    has_next, has_prev = me < n - 1, me > 0
+    outer = me + 2 * core - 1
+    has_outer = (outer >= 0) & (outer < n)
+    peers = [partner]
+    peers += [plane_peer(j)[1] for j in range(1, chips)]
+    peers += [(me + k * PLANE) % n for k in range(1, nz)]
+    barrier = pltpu.get_barrier_semaphore()
+    @pl.when(has_outer)
+    def _():
+        pl.semaphore_signal(barrier, inc=1, device_id=(outer,), device_id_type=MESH)
+
+    for peer in peers:
+        pl.semaphore_signal(barrier, inc=1, device_id=(peer,), device_id_type=MESH)
+
+    small = [
+        pltpu.make_async_copy(src, dst, small_sem.at[k])
+        for k, (src, dst) in enumerate((
+            (fh_h, fh), (fl_h, fl), (gh_h, gh), (gl_h, gl), (self_taps_h, self_taps), (fresh_h, fresh), (gate_h, gate),
+        ))
+    ]
+    for copy in small:
+        copy.start()
     loads = []
     for i in range(nz):
         for k, (src, dst) in enumerate(((hist, hist_v), (taps, taps_v))):
@@ -136,14 +158,7 @@
             copy.start()
             loads.append(copy)
 
-    outer = (me + 2 * core - 1 + n) % n
-    peers = [partner, outer]
-    peers += [plane_peer(j)[1] for j in range(1, chips)]
-    peers += [(me + k * PLANE) % n for k in range(1, nz)]
-    barrier = pltpu.get_barrier_semaphore()
-    for peer in peers:
-        pl.semaphore_signal(barrier, inc=1, device_id=(peer,), device_id_type=MESH)
-    pl.semaphore_wait(barrier, len(peers))
+    pl.semaphore_wait(barrier, len(peers) + jnp.where(has_outer, 1, 0))
 
     def taps_copy(i, z, dev):
         return remote(taps.at[pl.ds(rows - seg, seg), lanes(z, i)], tb.at[i], tb_s.at[i], tb_r.at[i], dev)
@@ -151,7 +166,6 @@
     def hist_copy(i, z, dev):
         return remote(hist.at[pl.ds(0, seg), lanes(z, i)], ha.at[i], ha_s.at[i], ha_r.at[i], dev)
 
-    has_next, has_prev = me < n - 1, me > 0
     for i in range(nz):
         @pl.when(has_next)
         def _(i=i):
@@ -182,6 +196,8 @@
     def _():
         ha[...] = jnp.zeros_like(ha)
 
+    for copy in small:
+        copy.wait()
     for i in range(nz):
         loads[2 * i].wait()
         loads[2 * i + 1].wait()
@@ -309,10 +325,12 @@
     spec = pltpu.VMEM((nz, 2 * seg, width), F32)
     return pl.pallas_call(
         lambda *refs: kernel(n, seg, *refs),
-        out_shape=jax.ShapeDtypeStruct(fresh.shape, F32),
-        in_specs=[hbm, hbm] + [vmem] * 7,
+        out_shape=pltpu.VMEM(fresh.shape, F32),
+        in_specs=[hbm] * 9,
         out_specs=vmem,
         scratch_shapes=[
+            pltpu.VMEM(fresh.shape, F32), pltpu.VMEM(fresh.shape, F32), pltpu.VMEM(fresh.shape, F32),
+            pltpu.VMEM(fh.shape, BF16), pltpu.VMEM(fh.shape, BF16), pltpu.VMEM(gh.shape, BF16), pltpu.VMEM(gh.shape, BF16),
             pltpu.VMEM((nz, rows, width), F32),
             pltpu.VMEM((nz, rows, width), F32),
             pltpu.VMEM((nz, seg, width), F32),
@@ -324,6 +342,7 @@
             pltpu.VMEM((nz, chips - 1, block, new_len), F32),
             pltpu.VMEM((nz, block, new_len), F32),
             pltpu.VMEM((nz - 1, block, new_len), F32),
+            dma((7,)),
             dma((2, nz)),
             dma((nz,)), dma((nz,)), dma((nz,)), dma((nz,)),
             dma((nz,)), dma((nz,)),

time: 32.9 us -> 30.5 us (0.927)
  Pallas kernels: 31.4 us -> 29.8 us
  local copies, waits for them, and re-layouts: 1.38 us -> 0.62 us
    pallas_call x1, Pallas kernels: 31.4 us -> 29.8 us  [kernel_body(): pl.pallas_call(lambda *refs: kernel(n, seg, *refs), out_shape=pltpu.VMEM(...]
    unnamed x1, local copies, waits for them, and re-layouts: 1.38 us -> 0.62 us
where the time goes in v1:
time: 30.5 us; the launch traced here: 30.4 us
  Pallas kernels  29.8 us (98%)
  local copies, waits for them, and re-layouts  0.62 us (2%)
    pallas_call x1, Pallas kernels, kernel_body(): pl.pallas_call(lambda *refs: kernel(n, seg, *refs), out_shape=pltpu.VMEM(...  29.8 us
    unnamed x1, local copies, waits for them, and re-layouts  0.62 us

profile of v1, /device:TPU:0, one launch (start us, length us, event | category | flops | bytes accessed | tf_op | source)
XLA Modules:
  0.0 30.4 jit_solution(5548391436290094866)
XLA Ops:
  0.0 29.8 %hyena.1 = f32[32,256]{1,0:T(8,128)S(1)} custom-call(f32[384,1024]{1,0:T(8,128)} %refs_0_.1, f32[384,1024]{1,0:T(8,128)} %refs_1_.1, f32[32,256]{1,0:T(8,128)} %refs_2_.1, f32[32,256]{1,0:T(8,128)} %refs_3_.1, f32[32,256]{1,0:T(8,128)} %refs_4_.1, bf16[256,256]{1,0:T(8,128)(2,1)} %constant.8.clone.refs_5_, bf16[256,256]{1,0:T(8,128)(2,1)} %constant.9.clone.refs_6_, ...), custom_call_target="tpu_custom_call" | custom-call | tf_op jit(solution)/shard_map/hyena/pallas_call | solution.py:326
  29.8 0.6 %copy.11 = f32[32,256]{1,0:T(8,128)} copy(f32[32,256]{1,0:T(8,128)S(1)} %hyena.1) | data formatting | bytes 65536

commit v2 on v1

--- a/solution.py
+++ b/solution.py
@@ -9,6 +9,7 @@
 from jax.sharding import PartitionSpec as P
 
 AXIS = "seq"
+DIRECT = 2
 PLANE = 8
 MESH = pl.DeviceIdType.MESH
 F32 = jnp.float32
@@ -103,26 +104,35 @@
 
 
 def kernel(n, seg, hist, taps, self_taps_h, fresh_h, gate_h, fh_h, fl_h, gh_h, gl_h, out,
-           self_taps, fresh, gate, fh, fl, gh, gl, hist_v, taps_v, tb, ha, sh0, sh1, st1, q0, q1, parts, d_recv, p_send, p_recv, z_send, z_recv,
-           small_sem, load_sem, tb_s, tb_r, ha_s, ha_r, d_s, d_r, p_s, p_r, z_s, z_r):
+           self_taps, fresh, gate, fh, fl, gh, gl, hist_v, taps_v, tb, ha, sh0, sh1, st1, q0, q1, parts, d_recv, sums, y_send, y_recv, w_send, w_recv,
+           p_recv, z_send, z_recv, x_send, x_recv,
+           small_sem, load_sem, tb_s, tb_r, ha_s, ha_r, d_s, d_r, y_s, y_r, w_s, w_r,
+           p_s, p_r, z_s, z_r, x_s, x_r):
     me = lax.axis_index(AXIS)
     nz = n // PLANE
     my_z, low = me // PLANE, me % PLANE
-    core, spot = me % 2, low // 2
+    core, x, y = me % 2, low // 2 % 2, low // 4
     rows = hist.shape[0]
     count = rows // seg
     width = hist.shape[1] // nz
     block = width // PLANE
     partner = me + 1 - 2 * core
-    chips = PLANE // 2
-
-    def lanes(z, i):
-        return pl.ds(pl.multiple_of(((z + 1 + i) % nz) * width, width), width)
-
-    def plane_peer(j):
-        bit0, bit1 = spot % 2, spot // 2
-        other = (bit0 + j % 2) % 2 + 2 * ((bit1 + j // 2) % 2)
-        return other, me - low + other * 2 + core
+    routed = nz - DIRECT
+    last = nz - 1
+    half = width // 2
+    x_peer, y_peer = me + 2 - 4 * x, me + 4 - 8 * y
+    diagonal = me + 2 - 4 * x + 4 - 8 * y
+    near = (y_peer, diagonal, x_peer)
+
+    def pieces(i, dev):
+        base = ((dev // PLANE + 1 + i) % nz) * width
+        if i < last:
+            return [(pl.ds(pl.multiple_of(base, width), width), pl.ds(0, width))]
+        row = dev % PLANE // 4
+        return [
+            (pl.ds(pl.multiple_of(base + ((row + 1 + h) % 2) * half, half), half), pl.ds(h * half, half))
+            for h in range(2)
+        ]
 
     def remote(src, dst, send, recv, dev):
         return pltpu.make_async_remote_copy(
@@ -133,7 +143,7 @@
     outer = me + 2 * core - 1
     has_outer = (outer >= 0) & (outer < n)
     peers = [partner]
-    peers += [plane_peer(j)[1] for j in range(1, chips)]
+    peers += near
     peers += [(me + k * PLANE) % n for k in range(1, nz)]
     barrier = pltpu.get_barrier_semaphore()
     @pl.when(has_outer)
@@ -151,29 +161,38 @@
     ]
     for copy in small:
         copy.start()
-    loads = []
+    loads = [[] for _ in range(nz)]
     for i in range(nz):
         for k, (src, dst) in enumerate(((hist, hist_v), (taps, taps_v))):
-            copy = pltpu.make_async_copy(src.at[:, lanes(my_z, i)], dst.at[i], load_sem.at[k, i])
-            copy.start()
-            loads.append(copy)
+            for h, (here, there) in enumerate(pieces(i, me)):
+                copy = pltpu.make_async_copy(src.at[:, here], dst.at[i, :, there], load_sem.at[k, i + h])
+                copy.start()
+                loads[i].append(copy)
 
     pl.semaphore_wait(barrier, len(peers) + jnp.where(has_outer, 1, 0))
 
-    def taps_copy(i, z, dev):
-        return remote(taps.at[pl.ds(rows - seg, seg), lanes(z, i)], tb.at[i], tb_s.at[i], tb_r.at[i], dev)
-
-    def hist_copy(i, z, dev):
-        return remote(hist.at[pl.ds(0, seg), lanes(z, i)], ha.at[i], ha_s.at[i], ha_r.at[i], dev)
+    def taps_copies(i, dev):
+        return [
+            remote(taps.at[pl.ds(rows - seg, seg), here], tb.at[i, :, there], tb_s.at[i + h], tb_r.at[i + h], dev)
+            for h, (here, there) in enumerate(pieces(i, dev))
+        ]
+
+    def hist_copies(i, dev):
+        return [
+            remote(hist.at[pl.ds(0, seg), here], ha.at[i, :, there], ha_s.at[i + h], ha_r.at[i + h], dev)
+            for h, (here, there) in enumerate(pieces(i, dev))
+        ]
 
     for i in range(nz):
         @pl.when(has_next)
         def _(i=i):
-            taps_copy(i, (me + 1) // PLANE, me + 1).start()
+            for copy in taps_copies(i, me + 1):
+                copy.start()
 
         @pl.when(has_prev)
         def _(i=i):
-            hist_copy(i, (me - 1) // PLANE, me - 1).start()
+            for copy in hist_copies(i, me - 1):
+                copy.start()
 
     def forward(value):
         both = jnp.concatenate(split(value), axis=0)
@@ -185,8 +204,8 @@
     def keep(ref, i, spec):
         ref[i, :seg], ref[i, seg:] = spec
 
-    def held(ref, i):
-        return ref[i, :seg], ref[i, seg:]
+    def held(ref, i, at):
+        return ref[i, :seg, at], ref[i, seg:, at]
 
     @pl.when(me == 0)
     def _():
@@ -199,8 +218,8 @@
     for copy in small:
         copy.wait()
     for i in range(nz):
-        loads[2 * i].wait()
-        loads[2 * i + 1].wait()
+        for copy in loads[i]:
+            copy.wait()
         hs = [forward(hist_v[i, pl.ds(a * seg, seg)]) for a in range(count)]
         ts = [forward(taps_v[i, pl.ds(a * seg, seg)]) for a in range(count)]
         first, second = local_products(hs, ts)
@@ -218,8 +237,8 @@
     f, s = fresh[...], self_taps[...]
     both = jnp.concatenate(split(jnp.concatenate([f[:, :seg], f[:, seg:], s[:, :seg], s[:, seg:]], axis=0)), axis=1)
     spec = dot_t(both, fh[...]) + dot_t(both, fl[...])
-    pieces = [(spec[k * block : (k + 1) * block, :seg], spec[k * block : (k + 1) * block, seg:]) for k in range(4)]
-    a, b = own_products(*pieces)
+    quads = [(spec[k * block : (k + 1) * block, :seg], spec[k * block : (k + 1) * block, seg:]) for k in range(4)]
+    a, b = own_products(*quads)
     high, low_half = split(jnp.concatenate([jnp.concatenate(a, axis=1), jnp.concatenate(b, axis=1)], axis=0))
     res = dot_t(high, gh[...]) + dot_t(low_half, gh[...]) + dot_t(high, gl[...])
     own = jnp.concatenate([res[:block], res[block:]], axis=1)
@@ -232,80 +251,131 @@
             + jnp.dot(gl[...], hi, preferred_element_type=F32)
         ).T
 
-    def chip_copy(i):
-        return remote(parts.at[i, 1 - core], d_recv.at[i], d_s.at[i], d_r.at[i], partner)
-
-    def plane_copy(i, j):
-        other, dev = plane_peer(j)
-        return remote(p_send.at[i, other], p_recv.at[i, j - 1], p_s.at[i, j - 1], p_r.at[i, j - 1], dev)
+    def chip_copy(i, h=None):
+        span, k = (pl.ds(0, 4), i) if h is None else (pl.ds(2 * h, 2), i + h)
+        return remote(parts.at[i, 1 - core, span], d_recv.at[i, span], d_s.at[k], d_r.at[k], partner)
+
+    def y_copy(i):
+        return remote(y_send.at[i], y_recv.at[i], y_s.at[i], y_r.at[i], y_peer)
+
+    def w_copy(i):
+        return remote(w_send.at[i], w_recv.at[i], w_s.at[i], w_r.at[i], (me + (i + 1) * PLANE) % n)
+
+    def near_copy(i, j):
+        k = i - routed
+        return remote(sums.at[k, (0, 1, 3)[j]], p_recv.at[k, j], p_s.at[k, j], p_r.at[k, j], near[j])
 
     def z_copy(i):
-        return remote(z_send.at[i], z_recv.at[i], z_s.at[i], z_r.at[i], (me + (i + 1) * PLANE) % n)
-
-    def step_compute(i):
+        k = i - routed
+        return remote(z_send.at[k], z_recv.at[k], z_s.at[k], z_r.at[k], (me + (i + 1) * PLANE) % n)
+
+    def x_copy():
+        return remote(x_send, x_recv, x_s, x_r, x_peer)
+
+    def compute(i, h=None):
+        which = slice(None) if h is None else slice(h, h + 1)
+
         @pl.when(has_prev)
         def _():
-            taps_copy(i, my_z, me).wait_recv()
+            for copy in taps_copies(i, me)[which]:
+                copy.wait_recv()
 
         @pl.when(has_next)
         def _():
-            hist_copy(i, my_z, me).wait_recv()
-
-        first, second = halo_products(
-            held(q0, i), held(q1, i), held(sh0, i), held(sh1, i), held(st1, i), forward(tb[i]), forward(ha[i])
+            for copy in hist_copies(i, me)[which]:
+                copy.wait_recv()
+
+        at = pl.ds(0, width) if h is None else pl.ds(h * half, half)
+        both = halo_products(
+            held(q0, i, at), held(q1, i, at), held(sh0, i, at), held(sh1, i, at), held(st1, i, at),
+            forward(tb[i, :, at]), forward(ha[i, :, at]),
         )
-        for half, spec in enumerate((first, second)):
+        for side, spec in enumerate(both):
             res = inverse(spec)
-            for p in range(chips):
-                for c in range(2):
-                    at = (p * 2 + c) * block
-                    parts[i, c, p, :, pl.ds(half * seg, seg)] = res[at : at + block]
-        chip_copy(i).start()
-
-    def step_plane(i):
+            for k in range(res.shape[0] // block):
+                col = k // 2 % 2
+                row = (k // 4 + y + 1) % 2 if h is None else h
+                place = 2 * row + (col + x) % 2
+                parts[i, k % 2, place, :, pl.ds(side * seg, seg)] = res[k * block : (k + 1) * block]
+        chip_copy(i, h).start()
+
+    def route_y(i):
         chip_copy(i).wait_recv()
-        p_send[i] = parts[i, core] + d_recv[i]
-        for j in range(1, chips):
-            plane_copy(i, j).start()
-
-    def step_z(i):
-        for j in range(1, chips):
-            plane_copy(i, j).wait_recv()
-        total = p_send[i, spot]
-        for j in range(1, chips):
-            total = total + p_recv[i, j - 1]
-        z_send[i] = total
-        if i < nz - 1:
-            z_copy(i).start()
-
-    for i in range(nz + 2):
-        if i < nz:
-            step_compute(i)
-        if 0 <= i - 1 < nz:
-            step_plane(i - 1)
-        if 0 <= i - 2 < nz:
-            step_z(i - 2)
-
-    total = z_send[nz - 1]
-    for i in range(nz - 1):
+        y_send[i] = parts[i, core, :2] + d_recv[i, :2]
+        y_copy(i).start()
+
+    def route_z(i):
+        y_copy(i).wait_recv()
+        w_send[i] = parts[i, core, 2:] + d_recv[i, 2:] + y_recv[i]
+        w_copy(i).start()
+
+    def spread(i, h=None):
+        chip_copy(i, h).wait_recv()
+        lo, hi = (0, 4) if h is None else (2 * h, 2 * h + 2)
+        sums[i - routed, lo:hi] = parts[i, core, lo:hi] + d_recv[i, lo:hi]
+        for j, place in enumerate((0, 1, 3)):
+            if lo <= place < hi:
+                near_copy(i, j).start()
+
+    def gathered(i):
+        for j in range(3):
+            near_copy(i, j).wait_recv()
+        k = i - routed
+        return sums[k, 2] + p_recv[k, 0] + p_recv[k, 1] + p_recv[k, 2]
+
+    for i in range(last):
+        compute(i)
+        if i < routed:
+            route_y(i)
+        else:
+            spread(i)
+        if 0 <= i - 1 < routed:
+            route_z(i - 1)
+    compute(last, 0)
+    if routed == last:
+        route_z(last - 1)
+    spread(last, 0)
+    compute(last, 1)
+    spread(last, 1)
+    for i in range(routed, last):
+        z_send[i - routed] = gathered(i)
+        z_copy(i).start()
+    for i in range(routed):
+        w_copy(i).wait_recv()
+    merged = w_recv[0]
+    for i in range(1, routed):
+        merged = merged + w_recv[i]
+    x_send[...] = merged[1]
+    x_copy().start()
+    total = gathered(last) + merged[0]
+    for i in range(routed, last):
         z_copy(i).wait_recv()
-        total = total + z_recv[i]
-    out[...] = gate[...] * (total + own)
-
+        total = total + z_recv[i - routed]
+    x_copy().wait_recv()
+    out[...] = gate[...] * (total + x_recv[...] + own)
+
+    x_copy().wait_send()
     for i in range(nz):
         @pl.when(has_next)
         def _(i=i):
-            taps_copy(i, (me + 1) // PLANE, me + 1).wait_send()
+            for copy in taps_copies(i, me + 1):
+                copy.wait_send()
 
         @pl.when(has_prev)
         def _(i=i):
-            hist_copy(i, (me - 1) // PLANE, me - 1).wait_send()
-
-        chip_copy(i).wait_send()
-        for j in range(1, chips):
-            plane_copy(i, j).wait_send()
-        if i < nz - 1:
-            z_copy(i).wait_send()
+            for copy in hist_copies(i, me - 1):
+                copy.wait_send()
+
+        for h in (None,) if i < last else (0, 1):
+            chip_copy(i, h).wait_send()
+        if i < routed:
+            y_copy(i).wait_send()
+            w_copy(i).wait_send()
+        else:
+            for j in range(3):
+                near_copy(i, j).wait_send()
+            if i < last:
+                z_copy(i).wait_send()
 
 
 def kernel_body(history, taps, self_taps, fresh, gate):
@@ -323,6 +393,7 @@
     chips = PLANE // 2
     dma = pltpu.SemaphoreType.DMA
     spec = pltpu.VMEM((nz, 2 * seg, width), F32)
+    pair = pltpu.VMEM((nz - DIRECT, 2, block, new_len), F32)
     return pl.pallas_call(
         lambda *refs: kernel(n, seg, *refs),
         out_shape=pltpu.VMEM(fresh.shape, F32),
@@ -338,16 +409,21 @@
             spec, spec, spec, spec, spec,
             pltpu.VMEM((nz, 2, chips, block, new_len), F32),
             pltpu.VMEM((nz, chips, block, new_len), F32),
-            pltpu.VMEM((nz, chips, block, new_len), F32),
-            pltpu.VMEM((nz, chips - 1, block, new_len), F32),
-            pltpu.VMEM((nz, block, new_len), F32),
-            pltpu.VMEM((nz - 1, block, new_len), F32),
+            pltpu.VMEM((DIRECT, chips, block, new_len), F32),
+            pair, pair, pair, pair,
+            pltpu.VMEM((DIRECT, 3, block, new_len), F32),
+            pltpu.VMEM((DIRECT, block, new_len), F32),
+            pltpu.VMEM((DIRECT, block, new_len), F32),
+            pltpu.VMEM((block, new_len), F32),
+            pltpu.VMEM((block, new_len), F32),
             dma((7,)),
-            dma((2, nz)),
+            dma((2, nz + 1)),
+            dma((nz + 1,)), dma((nz + 1,)), dma((nz + 1,)), dma((nz + 1,)),
+            dma((nz + 1,)), dma((nz + 1,)),
             dma((nz,)), dma((nz,)), dma((nz,)), dma((nz,)),
-            dma((nz,)), dma((nz,)),
-            dma((nz, chips - 1)), dma((nz, chips - 1)),
-            dma((nz - 1,)), dma((nz - 1,)),
+            dma((DIRECT, 3)), dma((DIRECT, 3)),
+            dma((DIRECT,)), dma((DIRECT,)),
+            dma, dma,
         ],
         compiler_params=pltpu.CompilerParams(collective_id=0, has_side_effects=True),
         name="hyena",
@@ -360,7 +436,7 @@
     def body(history, taps, self_taps, fresh, gate):
         channels = history.shape[1]
         block = fresh.shape[0]
-        fits = n % PLANE == 0 and n > PLANE and block % 8 == 0 and (block * PLANE) % 128 == 0
+        fits = n % PLANE == 0 and n > DIRECT * PLANE and block % 8 == 0 and (block * PLANE) % 256 == 0
         chosen = kernel_body if fits and channels == block * n else plain_body
         return chosen(history, taps, self_taps, fresh, gate)
 

time: 30.5 us -> 30.7 us (level)
  no operation moved by 1% of the time
where the time goes in v2:
time: 30.7 us; the launch traced here: 30.6 us
  Pallas kernels  29.9 us (97%)
  local copies, waits for them, and re-layouts  0.62 us (2%)
    pallas_call x1, Pallas kernels, kernel_body(): pl.pallas_call(lambda *refs: kernel(n, seg, *refs), out_shape=pltpu.VMEM(...  29.9 us
    unnamed x1, local copies, waits for them, and re-layouts  0.62 us

profile of v2, /device:TPU:0, one launch (start us, length us, event | category | flops | bytes accessed | tf_op | source)
XLA Modules:
  0.0 30.6 jit_solution(13109693148544533334)
XLA Ops:
  0.0 29.9 %hyena.1 = f32[32,256]{1,0:T(8,128)S(1)} custom-call(f32[384,1024]{1,0:T(8,128)} %refs_0_.1, f32[384,1024]{1,0:T(8,128)} %refs_1_.1, f32[32,256]{1,0:T(8,128)} %refs_2_.1, f32[32,256]{1,0:T(8,128)} %refs_3_.1, f32[32,256]{1,0:T(8,128)} %refs_4_.1, bf16[256,256]{1,0:T(8,128)(2,1)} %constant.8.clone.refs_5_, bf16[256,256]{1,0:T(8,128)(2,1)} %constant.9.clone.refs_6_, ...), custom_call_target="tpu_custom_call" | custom-call | tf_op jit(solution)/shard_map/hyena/pallas_call | solution.py:397
  29.9 0.6 %copy.11 = f32[32,256]{1,0:T(8,128)} copy(f32[32,256]{1,0:T(8,128)S(1)} %hyena.1) | data formatting | bytes 65536

commit v3 on v2

--- a/solution.py
+++ b/solution.py
@@ -9,7 +9,8 @@
 from jax.sharding import PartitionSpec as P
 
 AXIS = "seq"
-DIRECT = 2
+AHEAD = 3
+DIRECT = 3
 PLANE = 8
 MESH = pl.DeviceIdType.MESH
 F32 = jnp.float32
@@ -183,16 +184,19 @@
             for h, (here, there) in enumerate(pieces(i, dev))
         ]
 
-    for i in range(nz):
+    def send_halo(i):
         @pl.when(has_next)
-        def _(i=i):
+        def _():
             for copy in taps_copies(i, me + 1):
                 copy.start()
 
         @pl.when(has_prev)
-        def _(i=i):
+        def _():
             for copy in hist_copies(i, me - 1):
                 copy.start()
+
+    for i in range(min(AHEAD, nz)):
+        send_halo(i)
 
     def forward(value):
         both = jnp.concatenate(split(value), axis=0)
@@ -329,6 +333,8 @@
             route_y(i)
         else:
             spread(i)
+        if i + AHEAD < nz:
+            send_halo(i + AHEAD)
         if 0 <= i - 1 < routed:
             route_z(i - 1)
     compute(last, 0)
@@ -342,19 +348,23 @@
         z_copy(i).start()
     for i in range(routed):
         w_copy(i).wait_recv()
-    merged = w_recv[0]
-    for i in range(1, routed):
-        merged = merged + w_recv[i]
-    x_send[...] = merged[1]
-    x_copy().start()
-    total = gathered(last) + merged[0]
+    total = gathered(last)
+    if routed:
+        merged = w_recv[0]
+        for i in range(1, routed):
+            merged = merged + w_recv[i]
+        x_send[...] = merged[1]
+        x_copy().start()
+        total = total + merged[0]
     for i in range(routed, last):
         z_copy(i).wait_recv()
         total = total + z_recv[i - routed]
-    x_copy().wait_recv()
-    out[...] = gate[...] * (total + x_recv[...] + own)
-
-    x_copy().wait_send()
+    if routed:
+        x_copy().wait_recv()
+        total = total + x_recv[...]
+        x_copy().wait_send()
+    out[...] = gate[...] * (total + own)
+
     for i in range(nz):
         @pl.when(has_next)
         def _(i=i):
@@ -393,7 +403,7 @@
     chips = PLANE // 2
     dma = pltpu.SemaphoreType.DMA
     spec = pltpu.VMEM((nz, 2 * seg, width), F32)
-    pair = pltpu.VMEM((nz - DIRECT, 2, block, new_len), F32)
+    pair = pltpu.VMEM((max(nz - DIRECT, 1), 2, block, new_len), F32)
     return pl.pallas_call(
         lambda *refs: kernel(n, seg, *refs),
         out_shape=pltpu.VMEM(fresh.shape, F32),
@@ -436,7 +446,7 @@
     def body(history, taps, self_taps, fresh, gate):
         channels = history.shape[1]
         block = fresh.shape[0]
-        fits = n % PLANE == 0 and n > DIRECT * PLANE and block % 8 == 0 and (block * PLANE) % 256 == 0
+        fits = n % PLANE == 0 and n >= DIRECT * PLANE and block % 8 == 0 and (block * PLANE) % 256 == 0
         chosen = kernel_body if fits and channels == block * n else plain_body
         return chosen(history, taps, self_taps, fresh, gate)
 

time: 30.7 us -> 29.3 us (0.954)
  Pallas kernels: 29.9 us -> 28.6 us
    pallas_call x1, Pallas kernels: 29.9 us -> 28.6 us  [kernel_body(): pl.pallas_call(lambda *refs: kernel(n, seg, *refs), out_shape=pltpu.VMEM(...]
where the time goes in v3:
time: 29.3 us; the launch traced here: 29.2 us
  Pallas kernels  28.6 us (98%)
  local copies, waits for them, and re-layouts  0.62 us (2%)
    pallas_call x1, Pallas kernels, kernel_body(): pl.pallas_call(lambda *refs: kernel(n, seg, *refs), out_shape=pltpu.VMEM(...  28.6 us
    unnamed x1, local copies, waits for them, and re-layouts  0.62 us

profile of v3, /device:TPU:0, one launch (start us, length us, event | category | flops | bytes accessed | tf_op | source)
XLA Modules:
  0.0 29.2 jit_solution(3834305089269969572)
XLA Ops:
  0.0 28.6 %hyena.1 = f32[32,256]{1,0:T(8,128)S(1)} custom-call(f32[384,1024]{1,0:T(8,128)} %refs_0_.1, f32[384,1024]{1,0:T(8,128)} %refs_1_.1, f32[32,256]{1,0:T(8,128)} %refs_2_.1, f32[32,256]{1,0:T(8,128)} %refs_3_.1, f32[32,256]{1,0:T(8,128)} %refs_4_.1, bf16[256,256]{1,0:T(8,128)(2,1)} %constant.8.clone.refs_5_, bf16[256,256]{1,0:T(8,128)(2,1)} %constant.9.clone.refs_6_, ...), custom_call_target="tpu_custom_call" | custom-call | tf_op jit(solution)/shard_map/hyena/pallas_call | solution.py:407
  28.6 0.6 %copy.11 = f32[32,256]{1,0:T(8,128)} copy(f32[32,256]{1,0:T(8,128)S(1)} %hyena.1) | data formatting | bytes 65536

commit v4 on v3

--- a/solution.py
+++ b/solution.py
@@ -106,9 +106,9 @@
 
 def kernel(n, seg, hist, taps, self_taps_h, fresh_h, gate_h, fh_h, fl_h, gh_h, gl_h, out,
            self_taps, fresh, gate, fh, fl, gh, gl, hist_v, taps_v, tb, ha, sh0, sh1, st1, q0, q1, parts, d_recv, sums, y_send, y_recv, w_send, w_recv,
-           p_recv, z_send, z_recv, x_send, x_recv,
+           p_recv, z_send, z_recv, x_send, x_recv, f_recv,
            small_sem, load_sem, tb_s, tb_r, ha_s, ha_r, d_s, d_r, y_s, y_r, w_s, w_r,
-           p_s, p_r, z_s, z_r, x_s, x_r):
+           p_s, p_r, z_s, z_r, x_s, x_r, f_s, f_r):
     me = lax.axis_index(AXIS)
     nz = n // PLANE
     my_z, low = me // PLANE, me % PLANE
@@ -145,6 +145,7 @@
     has_outer = (outer >= 0) & (outer < n)
     peers = [partner]
     peers += near
+    peers += [(dev + n - last * PLANE) % n for dev in near]
     peers += [(me + k * PLANE) % n for k in range(1, nz)]
     barrier = pltpu.get_barrier_semaphore()
     @pl.when(has_outer)
@@ -276,6 +277,10 @@
     def x_copy():
         return remote(x_send, x_recv, x_s, x_r, x_peer)
 
+    def far_copy(place):
+        dev = ((y_peer, diagonal, me, x_peer)[place] + last * PLANE) % n
+        return remote(sums.at[last - 1 - routed, place], f_recv.at[place], f_s.at[place], f_r.at[place], dev)
+
     def compute(i, h=None):
         which = slice(None) if h is None else slice(h, h + 1)
 
@@ -317,6 +322,10 @@
         chip_copy(i, h).wait_recv()
         lo, hi = (0, 4) if h is None else (2 * h, 2 * h + 2)
         sums[i - routed, lo:hi] = parts[i, core, lo:hi] + d_recv[i, lo:hi]
+        if i == last - 1:
+            for place in range(4):
+                far_copy(place).start()
+            return
         for j, place in enumerate((0, 1, 3)):
             if lo <= place < hi:
                 near_copy(i, j).start()
@@ -343,7 +352,7 @@
     spread(last, 0)
     compute(last, 1)
     spread(last, 1)
-    for i in range(routed, last):
+    for i in range(routed, last - 1):
         z_send[i - routed] = gathered(i)
         z_copy(i).start()
     for i in range(routed):
@@ -356,9 +365,12 @@
         x_send[...] = merged[1]
         x_copy().start()
         total = total + merged[0]
-    for i in range(routed, last):
+    for i in range(routed, last - 1):
         z_copy(i).wait_recv()
         total = total + z_recv[i - routed]
+    for place in range(4):
+        far_copy(place).wait_recv()
+        total = total + f_recv[place]
     if routed:
         x_copy().wait_recv()
         total = total + x_recv[...]
@@ -381,10 +393,13 @@
         if i < routed:
             y_copy(i).wait_send()
             w_copy(i).wait_send()
+        elif i == last - 1:
+            for place in range(4):
+                far_copy(place).wait_send()
         else:
             for j in range(3):
                 near_copy(i, j).wait_send()
-            if i < last:
+            if i < last - 1:
                 z_copy(i).wait_send()
 
 
@@ -426,6 +441,7 @@
             pltpu.VMEM((DIRECT, block, new_len), F32),
             pltpu.VMEM((block, new_len), F32),
             pltpu.VMEM((block, new_len), F32),
+            pltpu.VMEM((4, block, new_len), F32),
             dma((7,)),
             dma((2, nz + 1)),
             dma((nz + 1,)), dma((nz + 1,)), dma((nz + 1,)), dma((nz + 1,)),
@@ -434,6 +450,7 @@
             dma((DIRECT, 3)), dma((DIRECT, 3)),
             dma((DIRECT,)), dma((DIRECT,)),
             dma, dma,
+            dma((4,)), dma((4,)),
         ],
         compiler_params=pltpu.CompilerParams(collective_id=0, has_side_effects=True),
         name="hyena",

time: 29.3 us -> 30.3 us (1.034)
  Pallas kernels: 28.6 us -> 29.5 us
    pallas_call x1, Pallas kernels: 28.6 us -> 29.5 us  [kernel_body(): pl.pallas_call(lambda *refs: kernel(n, seg, *refs), out_shape=pltpu.VMEM(...]
where the time goes in v4:
time: 30.3 us; the launch traced here: 30.1 us
  Pallas kernels  29.5 us (97%)
  local copies, waits for them, and re-layouts  0.62 us (2%)
    pallas_call x1, Pallas kernels, kernel_body(): pl.pallas_call(lambda *refs: kernel(n, seg, *refs), out_shape=pltpu.VMEM(...  29.5 us
    unnamed x1, local copies, waits for them, and re-layouts  0.62 us

profile of v4, /device:TPU:0, one launch (start us, length us, event | category | flops | bytes accessed | tf_op | source)
XLA Modules:
  0.0 30.1 jit_solution(16488502841844154635)
XLA Ops:
  0.0 29.5 %hyena.1 = f32[32,256]{1,0:T(8,128)S(1)} custom-call(f32[384,1024]{1,0:T(8,128)} %refs_0_.1, f32[384,1024]{1,0:T(8,128)} %refs_1_.1, f32[32,256]{1,0:T(8,128)} %refs_2_.1, f32[32,256]{1,0:T(8,128)} %refs_3_.1, f32[32,256]{1,0:T(8,128)} %refs_4_.1, bf16[256,256]{1,0:T(8,128)(2,1)} %constant.8.clone.refs_5_, bf16[256,256]{1,0:T(8,128)(2,1)} %constant.9.clone.refs_6_, ...), custom_call_target="tpu_custom_call" | custom-call | tf_op jit(solution)/shard_map/hyena/pallas_call | solution.py:422
  29.5 0.6 %copy.11 = f32[32,256]{1,0:T(8,128)} copy(f32[32,256]{1,0:T(8,128)S(1)} %hyena.1) | data formatting | bytes 65536

commit v5 on v3

--- a/solution.py
+++ b/solution.py
@@ -327,6 +327,10 @@
         k = i - routed
         return sums[k, 2] + p_recv[k, 0] + p_recv[k, 1] + p_recv[k, 2]
 
+    def send_z(i):
+        z_send[i - routed] = gathered(i)
+        z_copy(i).start()
+
     for i in range(last):
         compute(i)
         if i < routed:
@@ -337,15 +341,16 @@
             send_halo(i + AHEAD)
         if 0 <= i - 1 < routed:
             route_z(i - 1)
+        elif i - 1 >= routed:
+            send_z(i - 1)
     compute(last, 0)
     if routed == last:
         route_z(last - 1)
     spread(last, 0)
     compute(last, 1)
     spread(last, 1)
-    for i in range(routed, last):
-        z_send[i - routed] = gathered(i)
-        z_copy(i).start()
+    if routed < last:
+        send_z(last - 1)
     for i in range(routed):
         w_copy(i).wait_recv()
     total = gathered(last)

time: 29.3 us -> 30.7 us (1.048)
  Pallas kernels: 28.6 us -> 29.9 us
    pallas_call x1, Pallas kernels: 28.6 us -> 29.9 us  [kernel_body(): pl.pallas_call(lambda *refs: kernel(n, seg, *refs), out_shape=pltpu.VMEM(...]
where the time goes in v5:
time: 30.7 us; the launch traced here: 30.6 us
  Pallas kernels  29.9 us (97%)
  local copies, waits for them, and re-layouts  0.62 us (2%)
    pallas_call x1, Pallas kernels, kernel_body(): pl.pallas_call(lambda *refs: kernel(n, seg, *refs), out_shape=pltpu.VMEM(...  29.9 us
    unnamed x1, local copies, waits for them, and re-layouts  0.62 us

profile of v5, /device:TPU:0, one launch (start us, length us, event | category | flops | bytes accessed | tf_op | source)
XLA Modules:
  0.0 30.6 jit_solution(15464858926781393196)
XLA Ops:
  0.0 29.9 %hyena.1 = f32[32,256]{1,0:T(8,128)S(1)} custom-call(f32[384,1024]{1,0:T(8,128)} %refs_0_.1, f32[384,1024]{1,0:T(8,128)} %refs_1_.1, f32[32,256]{1,0:T(8,128)} %refs_2_.1, f32[32,256]{1,0:T(8,128)} %refs_3_.1, f32[32,256]{1,0:T(8,128)} %refs_4_.1, bf16[256,256]{1,0:T(8,128)(2,1)} %constant.8.clone.refs_5_, bf16[256,256]{1,0:T(8,128)(2,1)} %constant.9.clone.refs_6_, ...), custom_call_target="tpu_custom_call" | custom-call | tf_op jit(solution)/shard_map/hyena/pallas_call | solution.py:412
  29.9 0.6 %copy.11 = f32[32,256]{1,0:T(8,128)} copy(f32[32,256]{1,0:T(8,128)S(1)} %hyena.1) | data formatting | bytes 65536
